TPU v7x, 128 devices: a whole 4x4x4 slice. The times are simulated.
128 devices in a mesh: grp: 32 (over x, z, core), tp: 4 (over y).
Axes of the slice: x: 4, y: 4, z: 4, core: 2. Of those that a mesh axis runs over, the one named last changes fastest.
Arguments:
- q_nope: bfloat16 [2048, 16384], P('grp', 'tp'), may hold values from -6 to 6
- q_rope: bfloat16 [2048, 8192], P('grp', 'tp'), may hold values from -500 to 500
- w_uk: bfloat16 [128, 128, 512], P('tp'), may hold values from -0.5 to 0.5
- w_uv: bfloat16 [128, 512, 128], P('tp'), may hold values from -1 to 1
- prefix_latent: bfloat16 [64, 2048, 512], P('grp'), may hold values from -5 to 5
- prefix_rope: bfloat16 [64, 64, 2048], P('grp'), may hold values from -8 to 8
- suffix_latent: bfloat16 [2048, 256, 512], P(('grp', 'tp')), may hold values from -5 to 5
- suffix_rope: bfloat16 [2048, 64, 256], P(('grp', 'tp')), may hold values from -4 to 4
- suffix_len: int32 [32, 64], P('grp'), may hold values from 1 to 256, 8192 in all within a row
- request_prefix: int32 [2048], P('grp'), may hold values from 0 to 63, as said below
- prefix_slot: int32 [64], replicated, may hold values from 0 to 63, as said below
Outputs:
- attended: bfloat16 [2048, 16384], P('grp', 'tp')
Inputs may be any that keep to these rules, and one draw needn't show every extreme that they name: `request_prefix`: of the requests of one group, at most 2 name the same prefix; in every draw one prefix is named by exactly 2 requests of every group. `prefix_slot`: A permutation: each cache row holds exactly one prefix. `suffix_len`: the lengths of one group sum to 8192, and one of them is 256.
All inputs are finite; a program needn't handle non-finite values.
Results may differ from a plain program's by a relative error of at most 0.018.
Values may be sent and summed in bfloat16 or wider, within the bound.
A program may use at most 128 MiB of HBM per device.

v0:
```python
import math

import jax
import jax.numpy as jnp
from jax import lax
from jax.experimental import pallas as pl
from jax.experimental.pallas import tpu as pltpu
from jax.sharding import PartitionSpec as P

MESH = pl.DeviceIdType.MESH
BF, F32, I32 = jnp.bfloat16, jnp.float32, jnp.int32
LATENT, ROPE, NOPE, VALUE = 512, 64, 128, 128
PLEN, SLEN = 2048, 256
HEADS, REQS, OWN, GROUPS, TP = 32, 64, 16, 32, 4
SCALE = 1.0 / math.sqrt(NOPE + ROPE)
SCALE2 = SCALE * math.log2(math.e)
STATS = 128


def dot(a, b):
    return jnp.dot(a, b, preferred_element_type=F32)


def iota(shape, dim):
    return lax.broadcasted_iota(I32, shape, dim)


def onehot(mask):
    return jnp.where(mask, 1.0, 0.0).astype(BF)


def kernel(
    qn, qr, wuk, wuv, plat, prope, slat, srope, rp, ps, slen, out,
    qn_v, qr_v, wuk_v, wuv_v, pl_v, kt_v, sl_v, skr_v,
    sel_v, selt_v, perm_v, slots_v, slotst_v,
    xlat_v, yslat, yrlat, ysrope, yrrope, o_v, ybs, ybr, stat_v, ybs_st, ybr_st,
    xs, xr, qperm, vb, pst, bs0, br0, bs1, br1,
    qb0, qb1, s0, s1, pb0, pb1, out_v,
    lsem, osem, yss, yrs, yrss, yrrs, bss, brs, bsts, brts, xss, xrs, zss, zrs,
):
    g, t = lax.axis_index("grp"), lax.axis_index("tp")
    bar = pltpu.get_barrier_semaphore()
    for k in range(1, TP):
        pl.semaphore_signal(bar, inc=1, device_id=(g, lax.rem(t + k, TP)), device_id_type=MESH)

    def greet(k, c):
        pl.semaphore_signal(bar, inc=1, device_id=(lax.rem(g + k, GROUPS), t), device_id_type=MESH)
        return c

    lax.fori_loop(1, GROUPS, greet, 0)

    def rel(k):
        return pl.multiple_of(lax.rem(t + k, TP) * OWN, OWN)

    for k in range(TP):
        rows = pl.ds(k * OWN, OWN)
        pltpu.make_async_copy(qn.at[pl.ds(rel(k), OWN)], qn_v.at[rows], lsem.at[0]).start()
        pltpu.make_async_copy(qr.at[pl.ds(rel(k), OWN)], qr_v.at[rows], lsem.at[1]).start()
    loads = [(wuk, wuk_v)]
    for p in range(2):
        loads.append((plat.at[p], pl_v.at[p]))
        for b in range(2):
            loads.append((prope.at[p], kt_v.at[p, pl.ds(LATENT + b * ROPE, ROPE)]))
    loads.append((slat, sl_v))
    for b in range(2):
        loads.append((srope, skr_v.at[:, pl.ds(b * ROPE, ROPE)]))
    loads.append((wuv, wuv_v))
    copies = [pltpu.make_async_copy(a, b, lsem.at[2 + i]) for i, (a, b) in enumerate(loads)]
    for c in copies:
        c.start()
    ld_wuk, ld_p, ld_s, ld_wuv = copies[0], (copies[1:4], copies[4:7]), copies[7:10], copies[10]

    shift = lax.rem(128 - OWN * t, 128)
    named = pltpu.roll(rp[...].astype(F32), shift, 1)[0:1]
    sq = (128, 128)
    first = iota(sq, 0)
    slot_of = jnp.broadcast_to(ps[...].astype(F32)[0:1], sq).T
    hit = jnp.broadcast_to(named, sq) == first.astype(F32)
    slot = jnp.sum(jnp.where(hit, slot_of, 0.0), axis=0, keepdims=True)
    slot_b = jnp.broadcast_to(slot, sq)
    before = first < (iota(sq, 1) & 63)
    rank = jnp.sum(
        jnp.where(before & (slot_b.T == slot_b), 1.0, 0.0), axis=0, keepdims=True
    )
    buf = jnp.broadcast_to(2.0 * slot + rank, sq)
    buf_r = buf.astype(I32)
    buf_c = buf.T.astype(I32)
    for b in range(4):
        i, j = iota(sq, 0) + b * 128, iota(sq, 1)
        key, col = (i >> 4) * 4 + (i & 3), (i >> 2) & 3
        for e in range(2):
            sel_v[b * 128 : b * 128 + 128, e * 128 : e * 128 + 128] = onehot(
                (key == buf_r) & (col == ((j + e * 128) >> 6))
            )
        i, j = iota(sq, 0), iota(sq, 1) + b * 128
        key, col = (j >> 4) * 4 + (j & 3), (j >> 2) & 3
        for e in range(2):
            selt_v[e * 128 : e * 128 + 128, b * 128 : b * 128 + 128] = onehot(
                (key == buf_c) & (col == ((i + e * 128) >> 6))
            )
    i, j = iota((256, 256), 0), iota((256, 256), 1)
    perm_v[...] = onehot(j == (i & 15) * 16 + (i >> 4))
    for b in range(4):
        i, j = iota((128, 512), 0) + b * 128, iota((128, 512), 1)
        rows = pl.ds(b * 128, 128)
        slots_v[rows] = onehot(j == ((i >> 1) & 31) * 16 + (i >> 7) * 4 + ((i >> 6) & 1) * 2 + (i & 1))
        slotst_v[rows] = onehot(j == ((i >> 2) & 3) * 128 + ((i >> 1) & 1) * 64 + (i >> 4) * 2 + (i & 1))

    pltpu.make_async_copy(qn, qn_v, lsem.at[0]).wait()
    pltpu.make_async_copy(qr, qr_v, lsem.at[1]).wait()
    for hf in range(2):
        parts = []
        for src, wide in ((qn_v, 512), (qr_v, 256)):
            rhs = jnp.concatenate(
                [src[:, c * 2 * wide + hf * wide : c * 2 * wide + hf * wide + wide] for c in range(4)], axis=0
            )
            parts.append((rhs, wide))
        for (rhs, wide), at in zip(parts, (0, 512)):
            for b in range(4):
                got = dot(sel_v[b * 128 : b * 128 + 128], rhs).astype(BF)
                xs[hf, b * 8 : b * 8 + 8, :, at : at + wide] = got.reshape(8, 16, wide)

    def q_latents(par):
        def one(hp, c):
            h = 2 * hp + par
            q = qn_v[:, pl.ds(pl.multiple_of(h * NOPE, NOPE), NOPE)]
            y = dot(q, wuk_v[h]).astype(BF)
            for k in range(TP):
                xlat_v[k, hp] = y[k * OWN : k * OWN + OWN]
            return c

        lax.fori_loop(0, 16, one, 0, unroll=4)
        half = pl.ds(par * 16, 16)
        for k in range(TP):
            for n in range(2):
                z = dot(perm_v[...], xlat_v[k, :, :, n * 256 : n * 256 + 256].reshape(256, 256))
                z = z.astype(BF).reshape(16, 16, 256)
                if k == 0:
                    yrlat[0, :, half, n * 256 : n * 256 + 256] = z
                else:
                    yslat[k - 1, :, half, n * 256 : n * 256 + 256] = z

    for k in range(TP):
        rope = jnp.concatenate(
            [qr_v[k * OWN : k * OWN + OWN, hp * 128 : hp * 128 + 128] for hp in range(16)], axis=0
        )
        z = dot(perm_v[...], rope).astype(BF).reshape(16, 16, 128)
        if k == 0:
            yrrope[0] = z
        else:
            ysrope[k - 1] = z
    ld_wuk.wait()
    q_latents(0)

    def y_to(k):
        return (g, lax.rem(t + k, TP))

    def y_back(k):
        return (g, lax.rem(t + TP - k, TP))

    def y_copy(k, par, c):
        at = (pl.ds(c * 4, 4), pl.ds(par * 16, 16))
        n = (k - 1) * 8 + par * 4 + c
        return pltpu.make_async_remote_copy(
            src_ref=yslat.at[k - 1, at[0], at[1]],
            dst_ref=yrlat.at[k, at[0], at[1]],
            send_sem=yss.at[n], recv_sem=yrs.at[n], device_id=y_to(k), device_id_type=MESH,
        )

    def y_rope_copy(k):
        return pltpu.make_async_remote_copy(
            src_ref=ysrope.at[k - 1], dst_ref=yrrope.at[k],
            send_sem=yrss.at[k - 1], recv_sem=yrrs.at[k - 1], device_id=y_to(k), device_id_type=MESH,
        )

    def x_send(src, dst, ss, rs):
        def one(k, c):
            d = lax.rem(g + k, GROUPS)
            pltpu.make_async_remote_copy(
                src_ref=src.at[d], dst_ref=dst.at[g],
                send_sem=ss, recv_sem=rs, device_id=(d, t), device_id_type=MESH,
            ).start()
            return c

        lax.fori_loop(1, GROUPS, one, 0)

    def x_all(src, dst, ss, rs):
        many = pl.ds(0, GROUPS - 1)
        return pltpu.make_async_remote_copy(
            src_ref=src.at[many], dst_ref=dst.at[many],
            send_sem=ss, recv_sem=rs, device_id=(lax.rem(g + 1, GROUPS), t), device_id_type=MESH,
        )

    pl.semaphore_wait(bar, TP - 1 + GROUPS - 1)
    ropes = [y_rope_copy(k) for k in range(1, TP)]
    for c in ropes:
        c.start()
    ycs = {}
    for c in range(4):
        for k in range(1, TP):
            ycs[k, 0, c] = y_copy(k, 0, c)
            ycs[k, 0, c].start()
    for hf in range(2):
        x_send(xs.at[hf], xr.at[hf], xss.at[hf], xrs.at[hf])
        xr[hf, g] = xs[hf, g]
    q_latents(1)
    for c in range(4):
        for k in range(1, TP):
            ycs[k, 1, c] = y_copy(k, 1, c)
            ycs[k, 1, c].start()

    for p in range(2):
        for c in ld_p[p]:
            c.wait()

        def turn(j, c, p=p):
            at = pl.multiple_of(j * 256, 256)
            kt_v[p, 0:LATENT, pl.ds(at, 256)] = pl_v[p, pl.ds(at, 256), :].T
            return c

        lax.fori_loop(0, PLEN // 256, turn, 0)

    pst[...] = jnp.zeros_like(pst)
    stat_v[...] = jnp.zeros_like(stat_v)
    lane64 = iota((64, 128), 1)
    ld_wuv.wait()

    def prefix_block(hl, par, hf, qb, s, pb, p):
        for n in range(PLEN // 256):
            s[:, n * 256 : n * 256 + 256] = dot(qb[p], kt_v[p, :, n * 256 : n * 256 + 256])
        tops, sums = [], []
        for rc in range(8):
            rows = slice(rc * 32, rc * 32 + 32)
            top = s[rows, 0:128]
            for n in range(1, PLEN // 128):
                top = jnp.maximum(top, s[rows, n * 128 : n * 128 + 128])
            top = jnp.max(top, axis=1, keepdims=True)
            top_b = jnp.broadcast_to(top * SCALE2, (32, 128))
            total = jnp.zeros((32, 128), F32)
            for n in range(PLEN // 256):
                es = []
                for e in range(2):
                    at = n * 256 + e * 128
                    es.append(jnp.exp2(s[rows, at : at + 128] * SCALE2 - top_b))
                    total = total + es[e]
                pb[rows, n * 256 : n * 256 + 256] = jnp.concatenate(es, axis=1).astype(BF)
            tops.append(top)
            sums.append(jnp.sum(total, axis=1, keepdims=True))
        top, total = jnp.concatenate(tops, axis=0), jnp.concatenate(sums, axis=0)
        inv = 1.0 / total
        o = jnp.concatenate(
            [dot(pb[...], pl_v[p, :, n * 256 : n * 256 + 256]) * inv for n in range(2)], axis=1
        ).astype(BF)
        lse = top * SCALE + jnp.log(total)
        hi = lse.astype(BF).astype(F32)
        mid = (lse - hi).astype(BF).astype(F32)
        lo = lse - hi - mid
        for c in range(4):
            rows = slice(c * 64, c * 64 + 64)
            at = pl.ds(c * 128 + p * 64, 64)
            v = dot(o[rows], wuv_v[c * 8 + hl])
            vb[at, pl.ds(pl.multiple_of(hl * VALUE, VALUE), VALUE)] = v.astype(BF)
            row = pst[at]
            for n, part in enumerate((hi, mid, lo)):
                row = jnp.where(lane64 == hl * 3 + n, part[rows], row)
            pst[at] = row

    def prefix_half(hf):
        x_all(xs.at[hf], xr.at[hf], xss.at[hf], xrs.at[hf]).wait_recv()
        for b in range(4):
            for at in range(0, 768, 256):
                cut = xr[hf, :, :, at : at + 256].reshape(512, 256)
                qperm[b * 128 : b * 128 + 128, at : at + 256] = dot(
                    slots_v[b * 128 : b * 128 + 128], cut
                ).astype(BF)

        def pair(i, carry):
            for par, qb in ((0, qb0), (1, qb1)):
                hl = hf * 4 + i * 2 + par
                for c in range(4):
                    q = qperm[c * 128 : c * 128 + 128, pl.ds(pl.multiple_of((i * 2 + par) * 128, 128), 128)]
                    y = dot(q, wuk_v[c * 8 + hl]).astype(BF)
                    r = qperm[c * 128 : c * 128 + 128, pl.ds(pl.multiple_of(512 + i * 128, 128), 128)]
                    lane = iota((128, 128), 1)
                    r = jnp.where((lane < 64) if par == 0 else (lane >= 64), r, jnp.zeros_like(r))
                    for p in range(2):
                        rows = pl.ds(c * 64, 64)
                        qb[p, rows, 0:LATENT] = y[p * 64 : p * 64 + 64]
                        qb[p, rows, LATENT : LATENT + 128] = r[p * 64 : p * 64 + 64]
            for par, qb in ((0, qb0), (1, qb1)):
                hl = hf * 4 + i * 2 + par
                prefix_block(hl, par, hf, qb, s0, pb0, 0)
                prefix_block(hl, par, hf, qb, s1, pb1, 1)
            return carry

        lax.fori_loop(0, 2, pair, 0)

    prefix_half(0)
    for b in range(4):
        z = dot(slotst_v[b * 128 : b * 128 + 128], vb[:, 0:512])
        bs0[b * 8 : b * 8 + 8] = z.astype(BF).reshape(8, 16, 512)
    x_send(bs0, br0, zss.at[0], zrs.at[0])
    br0[g] = bs0[g]

    for c in ld_s:
        c.wait()
    for c in ropes:
        c.wait_recv()
    srow, slane = iota((128, 128), 0), iota((128, 128), 1)

    def suffix_one(r, carry):
        ql = jnp.concatenate([yrlat[k, r] for k in range(TP)], axis=0)
        lane = iota((16, 128), 1)
        parts = []
        for k in range(TP):
            x = yrrope[k, r]
            parts += [jnp.where(lane < 64, x, jnp.zeros_like(x)), jnp.where(lane >= 64, x, jnp.zeros_like(x))]
        kv = sl_v[r]
        s = lax.dot_general(ql, kv, (((1,), (1,)), ((), ())), preferred_element_type=F32)
        s = s + dot(jnp.concatenate(parts, axis=0), skr_v[r])
        live = iota((128, SLEN), 1) < slen[0, t * OWN + r]
        s = jnp.where(live, s, -1e30)
        top = jnp.max(s, axis=1, keepdims=True)
        e = jnp.where(live, jnp.exp2((s - top) * SCALE2), 0.0)
        total = jnp.sum(e, axis=1, keepdims=True)
        o = (dot(e.astype(BF), kv) * (1.0 / total)).astype(BF)
        for k in range(TP):
            for par in range(2):
                at = (k * 2 + par) * 16
                o_v[k, par, r] = o[at : at + 16]
        lse = top * SCALE + jnp.log(total)
        stat_v[...] = jnp.where(slane == (srow >> 5) * OWN + r, lse, stat_v[...])
        return carry

    for c in range(4):
        for par in range(2):
            for k in range(1, TP):
                ycs[k, par, c].wait_recv()
        lax.fori_loop(c * 4, c * 4 + 4, suffix_one, 0, unroll=2)

    def yb_copy(k, q):
        at = pl.ds(q * 4, 4)
        n = (k - 1) * 4 + q
        return pltpu.make_async_remote_copy(
            src_ref=ybs.at[k - 1, at], dst_ref=ybr.at[k, at],
            send_sem=bss.at[n], recv_sem=brs.at[n], device_id=y_back(k), device_id_type=MESH,
        )

    def yb_stat_copy(k):
        return pltpu.make_async_remote_copy(
            src_ref=ybs_st.at[k - 1], dst_ref=ybr_st.at[k],
            send_sem=bsts.at[k - 1], recv_sem=brts.at[k - 1], device_id=y_back(k), device_id_type=MESH,
        )

    for k in range(TP):
        part = stat_v[k * 32 : k * 32 + 32]
        if k == 0:
            ybr_st[0] = part
        else:
            ybs_st[k - 1] = part
    stats = [yb_stat_copy(k) for k in range(1, TP)]
    for c in stats:
        c.start()
    backs = {}
    for q in range(4):
        for k in range(TP):
            for par in range(2):
                for n in range(2):
                    cut = o_v[k, par, :, :, n * 256 : n * 256 + 256].reshape(256, 256)
                    z = dot(perm_v[q * 64 : q * 64 + 64], cut).astype(BF).reshape(4, 16, 256)
                    if k == 0:
                        ybr[0, q * 4 : q * 4 + 4, par, :, n * 256 : n * 256 + 256] = z
                    else:
                        ybs[k - 1, q * 4 : q * 4 + 4, par, :, n * 256 : n * 256 + 256] = z
            if k:
                backs[k, q] = yb_copy(k, q)
                backs[k, q].start()

    prefix_half(1)
    vb[:, 1024 : 1024 + STATS] = pst[...].astype(BF)
    for b in range(4):
        z = dot(slotst_v[b * 128 : b * 128 + 128], vb[:, 512 : 1024 + STATS])
        bs1[b * 8 : b * 8 + 8] = z.astype(BF).reshape(8, 16, 512 + STATS)
    x_send(bs1, br1, zss.at[1], zrs.at[1])
    br1[g] = bs1[g]

    x_all(bs0, br0, zss.at[0], zrs.at[0]).wait_recv()
    x_all(bs1, br1, zss.at[1], zrs.at[1]).wait_recv()
    for c in stats:
        c.wait_recv()
    st = ybr_st[0] + ybr_st[1] + ybr_st[2] + ybr_st[3]
    st = jnp.concatenate([st, jnp.zeros((96, 128), F32)], axis=0).T
    outs = []
    for q in range(4):
        rows = selt_v[q * 64 : q * 64 + 64]
        pv = (dot(rows, br0[...].reshape(512, 512)), dot(rows, br1[...].reshape(512, 512 + STATS)))
        for k in range(1, TP):
            backs[k, q].wait_recv()
        for hl in range(8):
            h = q * 8 + hl
            hp, par = h // 2, h % 2
            lhs = jnp.concatenate([ybr[k, hp, par] for k in range(TP)], axis=0)
            sv = dot(lhs, wuv_v[h]).astype(BF).astype(F32)
            at = (hl % 4) * 128
            prefix = pv[hl // 4][:, at : at + 128]
            lp = pv[1][:, 512 + hl * 3 : 512 + hl * 3 + 1]
            for n in range(1, 3):
                lp = lp + pv[1][:, 512 + hl * 3 + n : 512 + hl * 3 + n + 1]
            ls = st[0:64, par * 16 + hp : par * 16 + hp + 1]
            top = jnp.maximum(lp, ls)
            a, b = jnp.exp(lp - top), jnp.exp(ls - top)
            inv = 1.0 / (a + b)
            out_v[:, h * 128 : h * 128 + 128] = ((a * inv) * prefix + (b * inv) * sv).astype(BF)
        for k in range(TP):
            c = pltpu.make_async_copy(
                out_v.at[pl.ds(k * OWN, OWN), pl.ds(q * 1024, 1024)],
                out.at[pl.ds(rel(k), OWN), pl.ds(q * 1024, 1024)],
                osem.at[q * 4 + k],
            )
            c.start()
            outs.append(c)
    for c in outs:
        c.wait()
    for c in (*ropes, *ycs.values(), *backs.values(), *stats):
        c.wait_send()
    for hf in range(2):
        x_all(xs.at[hf], xr.at[hf], xss.at[hf], xrs.at[hf]).wait_send()
    x_all(bs0, br0, zss.at[0], zrs.at[0]).wait_send()
    x_all(bs1, br1, zss.at[1], zrs.at[1]).wait_send()


def local(qn, qr, wuk, wuv, plat, prope, slat, srope, slen, named, slot):
    rp = jnp.broadcast_to(jnp.tile(named, 2)[None], (8, 128))
    ps = jnp.broadcast_to(jnp.tile(slot, 2)[None], (8, 128))
    hbm = pl.BlockSpec(memory_space=pl.ANY)
    vmem = pl.BlockSpec(memory_space=pltpu.VMEM)
    smem = pl.BlockSpec(memory_space=pltpu.SMEM)

    def b(*shape):
        return pltpu.VMEM(shape, BF)

    def f(*shape):
        return pltpu.VMEM(shape, F32)

    def sem(n):
        return pltpu.SemaphoreType.DMA((n,))

    return pl.pallas_call(
        kernel,
        out_shape=jax.ShapeDtypeStruct((REQS, HEADS * VALUE), BF),
        in_specs=[hbm] * 8 + [vmem, vmem, smem],
        out_specs=hbm,
        scratch_shapes=[
            b(64, 4096), b(64, 2048), b(32, 128, 512), b(32, 512, 128), b(2, 2048, 512), b(2, 640, 2048),
            b(16, 256, 512), b(16, 128, 256),
            b(512, 256), b(256, 512), b(256, 256), b(512, 512), b(512, 512),
            b(4, 16, 16, 512), b(3, 16, 32, 512), b(4, 16, 32, 512), b(3, 16, 16, 128), b(4, 16, 16, 128),
            b(4, 2, 16, 16, 512), b(3, 16, 2, 16, 512), b(4, 16, 2, 16, 512),
            f(128, 128), f(3, 32, 128), f(4, 32, 128),
            b(2, 32, 16, 768), b(2, 32, 16, 768), b(512, 768), b(512, 1024 + STATS), f(512, 128),
            b(32, 16, 512), b(32, 16, 512), b(32, 16, 512 + STATS), b(32, 16, 512 + STATS),
            b(2, 256, 640), b(2, 256, 640), f(256, 2048), f(256, 2048), b(256, 2048), b(256, 2048),
            b(64, 4096),
            sem(13), sem(16), sem(24), sem(24), sem(3), sem(3), sem(12), sem(12), sem(3), sem(3),
            sem(2), sem(2), sem(2), sem(2),
        ],
        compiler_params=pltpu.CompilerParams(
            collective_id=0, has_side_effects=True, vmem_limit_bytes=67043328
        ),
        name="attend",
    )(qn, qr, wuk, wuv, plat, prope, slat, srope, rp, ps, slen)


def solution(mesh):
    in_specs = (
        P("grp", "tp"), P("grp", "tp"), P("tp", None, None), P("tp", None, None),
        P("grp", None, None), P("grp", None, None), P(("grp", "tp"), None, None), P(("grp", "tp"), None, None),
        P("grp", None), P("grp"), P(),
    )
    return jax.shard_map(local, mesh=mesh, in_specs=in_specs, out_specs=P("grp", "tp"), check_vma=False)
```

profile of v0, /device:TPU:1, one launch (start us, length us, event | category | flops | bytes accessed | tf_op | source)
XLA Modules:
  0.0 91.2 jit_solution(4299262583242751090)
XLA Ops:
  0.0 0.7 tile.4
  0.7 0.1 broadcast_in_dim.14
  0.7 0.7 tile.5
  1.4 0.1 broadcast_in_dim.16
  1.5 0.6 broadcast_in_dim.17.ps
  2.1 0.6 broadcast_in_dim.15.rp
  2.7 86.6 %attend.1 = bf16[64,4096]{1,0:T(8,128)(2,1)} custom-call(bf16[64,4096]{1,0:T(8,128)(2,1)} %qn.1, bf16[64,2048]{1,0:T(8,128)(2,1)} %qr.1, bf16[32,128,512]{2,1,0:T(8,128)(2,1)} %wuk.1, bf16[32,512,128]{2,1,0:T(8,128)(2,1)} %wuv.1, bf16[2,2048,512]{2,1,0:T(8,128)(2,1)} %plat.1, bf16[2,64,2048]{2,1,0:T(8,128)(2,1)} %prope.1, bf16[16,256,512]{2,1,0:T(8,128)(2,1)} %slat.1, ...), custom_call_target="tpu_custom_call" | custom-call | tf_op jit(solution)/shard_map/attend/pallas_call | solution.py:448
  89.3 1.9 %copy.13 = bf16[64,4096]{1,0:T(8,128)(2,1)} copy(bf16[64,4096]{1,0:T(8,128)(2,1)} %attend.1) | data formatting | bytes 1048576
where the time goes:
time: 92 us; the launch traced here: 91.2 us
  Pallas kernels  86.6 us (94%)
  local copies, waits for them, and re-layouts  4.54 us (5%)
    pallas_call x1, Pallas kernels, local(): pl.pallas_call(kernel, out_shape=jax.ShapeDtypeStruct((REQS, HEADS * VALU...  86.6 us
    unnamed x1, local copies, waits for them, and re-layouts  1.87 us

commit v1 on v0

v1 whole, which is shorter than its diff:
```python
import math

import jax
import jax.numpy as jnp
from jax import lax
from jax.experimental import pallas as pl
from jax.experimental.pallas import tpu as pltpu
from jax.sharding import PartitionSpec as P

MESH = pl.DeviceIdType.MESH
BF, F32, I32 = jnp.bfloat16, jnp.float32, jnp.int32
LATENT, ROPE, NOPE, VALUE = 512, 64, 128, 128
PLEN, SLEN = 2048, 256
HEADS, REQS, OWN, GROUPS, TP = 32, 64, 16, 32, 4
SCALE = 1.0 / math.sqrt(NOPE + ROPE)
SCALE2 = SCALE * math.log2(math.e)
QUARTERS = 4
STATS = 128


def dot(a, b):
    return jnp.dot(a, b, preferred_element_type=F32)


def iota(shape, dim):
    return lax.broadcasted_iota(I32, shape, dim)


def onehot(mask):
    return jnp.where(mask, 1.0, 0.0).astype(BF)


def kernel(
    qn, qr, wuk, wuv, plat, prope, slat, srope, rp, ps, slen, out,
    qn_v, qr_v, wuk_v, wuv_v, pl_v, kt_v, sl_v, skr_v,
    sel_v, selt_v, perm_v, permb_v, slots_v, slotst_v,
    xlat_v, yslat, yrlat, ysrope, yrrope, o_v, ybs, ybr, stat_v, ybs_st, ybr_st,
    xs, xr, qp, vq, pst, bs, br, bs_st, br_st,
    qb, sc, pb, ob, ss, es, pv_v, sv_v, out_v,
    lsem, osem, yss, yrs, yrss, yrrs, bss, brs, bsts, brts, xss, xrs, zss, zrs,
):
    g, t = lax.axis_index("grp"), lax.axis_index("tp")
    def rel(k):
        return pl.multiple_of(lax.rem(t + k, TP) * OWN, OWN)

    for k in range(TP):
        rows = pl.ds(k * OWN, OWN)
        pltpu.make_async_copy(qn.at[pl.ds(rel(k), OWN)], qn_v.at[rows], lsem.at[0]).start()
        pltpu.make_async_copy(qr.at[pl.ds(rel(k), OWN)], qr_v.at[rows], lsem.at[1]).start()
    loads = [(wuk, wuk_v)]
    for p in range(2):
        loads.append((plat.at[p], pl_v.at[p]))
        for b in range(2):
            loads.append((prope.at[p], kt_v.at[p, pl.ds(LATENT + b * ROPE, ROPE)]))
    loads.append((slat, sl_v))
    for b in range(2):
        loads.append((srope, skr_v.at[:, pl.ds(b * ROPE, ROPE)]))
    loads.append((wuv, wuv_v))
    copies = [pltpu.make_async_copy(a, b, lsem.at[2 + i]) for i, (a, b) in enumerate(loads)]
    copies[0].start()
    bar = pltpu.get_barrier_semaphore()
    for k in range(1, TP):
        pl.semaphore_signal(bar, inc=1, device_id=(g, lax.rem(t + k, TP)), device_id_type=MESH)

    def greet(k, c):
        pl.semaphore_signal(bar, inc=1, device_id=(lax.rem(g + k, GROUPS), t), device_id_type=MESH)
        return c

    lax.fori_loop(1, GROUPS, greet, 0)

    for c in copies[1:]:
        c.start()
    ld_wuk, ld_p, ld_s, ld_wuv = copies[0], (copies[1:4], copies[4:7]), copies[7:10], copies[10]

    i, j = iota((256, 256), 0), iota((256, 256), 1)
    perm_v[...] = onehot(j == (i & 15) * 16 + (i >> 4))

    def q_latents(par):
        def one(hp, c):
            h = 2 * hp + par
            q = qn_v[:, pl.ds(pl.multiple_of(h * NOPE, NOPE), NOPE)]
            y = dot(q, wuk_v[h]).astype(BF)
            for k in range(TP):
                xlat_v[k, hp] = y[k * OWN : k * OWN + OWN]
            return c

        lax.fori_loop(0, 16, one, 0, unroll=4)
        half = pl.ds(par * 16, 16)
        for k in range(TP):
            for n in range(2):
                z = dot(perm_v[...], xlat_v[k, :, :, n * 256 : n * 256 + 256].reshape(256, 256))
                z = z.astype(BF).reshape(16, 16, 256)
                if k == 0:
                    yrlat[0, :, half, n * 256 : n * 256 + 256] = z
                else:
                    yslat[k - 1, :, half, n * 256 : n * 256 + 256] = z

    with jax.named_scope("wait_q"):
        pltpu.make_async_copy(qn, qn_v, lsem.at[0]).wait()
        pltpu.make_async_copy(qr, qr_v, lsem.at[1]).wait()
    with jax.named_scope("ropes"):
        for k in range(TP):
            rope = jnp.concatenate(
                [qr_v[k * OWN : k * OWN + OWN, hp * 128 : hp * 128 + 128] for hp in range(16)], axis=0
            )
            z = dot(perm_v[...], rope).astype(BF).reshape(16, 16, 128)
            if k == 0:
                yrrope[0] = z
            else:
                ysrope[k - 1] = z
    ld_wuk.wait()
    with jax.named_scope("qlat0"):
        q_latents(0)

    def y_to(k):
        return (g, lax.rem(t + k, TP))

    def y_back(k):
        return (g, lax.rem(t + TP - k, TP))

    def y_copy(k, par, c):
        at = (pl.ds(c * 4, 4), pl.ds(par * 16, 16))
        n = (k - 1) * 8 + par * 4 + c
        return pltpu.make_async_remote_copy(
            src_ref=yslat.at[k - 1, at[0], at[1]],
            dst_ref=yrlat.at[k, at[0], at[1]],
            send_sem=yss.at[n], recv_sem=yrs.at[n], device_id=y_to(k), device_id_type=MESH,
        )

    def y_rope_copy(k):
        return pltpu.make_async_remote_copy(
            src_ref=ysrope.at[k - 1], dst_ref=yrrope.at[k],
            send_sem=yrss.at[k - 1], recv_sem=yrrs.at[k - 1], device_id=y_to(k), device_id_type=MESH,
        )

    def x_send(src, dst, ss, rs):
        def one(k, c):
            d = lax.rem(g + k, GROUPS)
            pltpu.make_async_remote_copy(
                src_ref=src.at[d], dst_ref=dst.at[g],
                send_sem=ss, recv_sem=rs, device_id=(d, t), device_id_type=MESH,
            ).start()
            return c

        lax.fori_loop(1, GROUPS, one, 0)
        dst[g] = src[g]

    def x_all(src, dst, ss, rs):
        many = pl.ds(0, GROUPS - 1)
        return pltpu.make_async_remote_copy(
            src_ref=src.at[many], dst_ref=dst.at[many],
            send_sem=ss, recv_sem=rs, device_id=(lax.rem(g + 1, GROUPS), t), device_id_type=MESH,
        )

    def forward(i):
        return xs.at[i], xr.at[i], xss.at[i], xrs.at[i]

    def backward(i):
        return bs.at[i], br.at[i], zss.at[i], zrs.at[i]

    back_stats = (bs_st, br_st, zss.at[QUARTERS], zrs.at[QUARTERS])

    with jax.named_scope("barrier"):
        pl.semaphore_wait(bar, TP - 1 + GROUPS - 1)
    ropes = [y_rope_copy(k) for k in range(1, TP)]
    for c in ropes:
        c.start()
    for k in range(1, TP):
        y_copy(k, 0, 0).start()
    with jax.named_scope("route"):
        sq = (128, 128)
        first = iota(sq, 0)
        lane1 = iota((1, 128), 1) & 63
        slot = jnp.zeros((1, 128), I32)
        for j in range(REQS):
            slot = jnp.where(lane1 == j, ps[rp[lax.rem(t * OWN + j, REQS)]], slot)
        slot = slot.astype(F32)
        slot_b = jnp.broadcast_to(slot, sq)
        before = first < (iota(sq, 1) & 63)
        rank = jnp.sum(jnp.where(before & (slot_b.T == slot_b), 1.0, 0.0), axis=0, keepdims=True)
        buf = jnp.broadcast_to(2.0 * slot + rank, sq)
        buf_r = buf.astype(I32)
        buf_c = buf.T.astype(I32)
        for b in range(4):
            i, j = iota(sq, 0) + b * 128, iota(sq, 1)
            key, col = (i >> 4) * 4 + (i & 3), (i >> 2) & 3
            for e in range(2):
                sel_v[b * 128 : b * 128 + 128, e * 128 : e * 128 + 128] = onehot(
                    (key == buf_r) & (col == ((j + e * 128) >> 6))
                )

    with jax.named_scope("place"):
        for hf in range(QUARTERS):
            for src, wide, at in ((qn_v, 256, 0), (qr_v, 128, 256)):
                rhs = jnp.concatenate(
                    [src[:, (c * 4 + hf) * wide : (c * 4 + hf) * wide + wide] for c in range(4)], axis=0
                )
                for b in range(4):
                    got = dot(sel_v[b * 128 : b * 128 + 128], rhs).astype(BF)
                    xs[hf, b * 8 : b * 8 + 8, :, at : at + wide] = got.reshape(8, 16, wide)
            x_send(*forward(hf))
    with jax.named_scope("qlat1"):
        q_latents(1)
    for c in range(4):
        for par in range(2):
            for k in range(1, TP):
                if c or par:
                    y_copy(k, par, c).start()

    with jax.named_scope("masks"):
        for b in range(4):
            i, j = iota((128, 512), 0) + b * 128, iota((128, 512), 1)
            rows = pl.ds(b * 128, 128)
            slots_v[rows] = onehot(j == ((i >> 1) & 31) * 16 + (i >> 7) * 4 + ((i >> 6) & 1) * 2 + (i & 1))
            slotst_v[rows] = onehot(
                j == ((i >> 2) & 3) * 128 + ((i >> 1) & 1) * 64 + (i >> 4) * 2 + (i & 1)
            )
            i, j = iota(sq, 0), iota(sq, 1) + b * 128
            key, col = (j >> 4) * 4 + (j & 3), (j >> 2) & 3
            for e in range(2):
                selt_v[e * 128 : e * 128 + 128, b * 128 : b * 128 + 128] = onehot(
                    (key == buf_c) & (col == ((i + e * 128) >> 6))
                )
        i, j = iota((256, 256), 0), iota((256, 256), 1)
        permb_v[...] = onehot(j == (i & 7) * 32 + ((i >> 3) & 1) * 16 + (i >> 4))

    with jax.named_scope("turn"):
        for p in range(2):
            for c in ld_p[p]:
                c.wait()

            def turn(j, c, p=p):
                at = pl.multiple_of(j * 256, 256)
                kt_v[p, 0:LATENT, pl.ds(at, 256)] = pl_v[p, pl.ds(at, 256), :].T
                return c

            lax.fori_loop(0, PLEN // 256, turn, 0)

    pst[...] = jnp.zeros_like(pst)
    stat_v[...] = jnp.zeros_like(stat_v)
    lane64 = iota((64, 128), 1)
    with jax.named_scope("loads"):
        ld_wuv.wait()
        for c in ld_s:
            c.wait()

    def scores(b, n):
        at = pl.ds(n * 256, 256)
        sc[b % 2, :, at] = dot(qb[b], kt_v[b % 2, :, at])

    def weigh(b, n):
        rows = slice(n * 32, n * 32 + 32)
        s = sc.at[b % 2]
        top = s[rows, 0:128]
        for m in range(1, PLEN // 128):
            top = jnp.maximum(top, s[rows, m * 128 : m * 128 + 128])
        top = jnp.max(top, axis=1, keepdims=True)
        top_b = jnp.broadcast_to(top * SCALE2, (32, 128))
        total = jnp.zeros((32, 128), F32)
        for m in range(PLEN // 256):
            e = [
                jnp.exp2(s[rows, at : at + 128] * SCALE2 - top_b)
                for at in (m * 256, m * 256 + 128)
            ]
            total = total + e[0] + e[1]
            pb[b % 2, rows, m * 256 : m * 256 + 256] = jnp.concatenate(e, axis=1).astype(BF)
        return top, jnp.sum(total, axis=1, keepdims=True)

    def values(b, n, inv):
        at = pl.ds(n * 256, 256)
        ob[b % 2, :, at] = (dot(pb[b % 2], pl_v[b % 2, :, at]) * inv).astype(BF)

    def quarter(i):
        with jax.named_scope("wait_x"):
            x_all(*forward(i)).wait_recv()
        for b in range(4):
            for at, wide in ((0, 256), (256, 128)):
                cut = xr[i, :, :, at : at + wide].reshape(512, wide)
                qp[b * 128 : b * 128 + 128, at : at + wide] = dot(
                    slots_v[b * 128 : b * 128 + 128], cut
                ).astype(BF)
        lane = iota((128, 128), 1)
        for par in range(2):
            for c in range(4):
                rows = slice(c * 128, c * 128 + 128)
                y = dot(qp[rows, par * 128 : par * 128 + 128], wuk_v[c * 8 + 2 * i + par]).astype(BF)
                r = qp[rows, 256:384]
                r = jnp.where((lane < 64) if par == 0 else (lane >= 64), r, jnp.zeros_like(r))
                for p in range(2):
                    qb[par * 2 + p, c * 64 : c * 64 + 64, 0:LATENT] = y[p * 64 : p * 64 + 64]
                    qb[par * 2 + p, c * 64 : c * 64 + 64, LATENT : LATENT + 128] = r[p * 64 : p * 64 + 64]
        inv = {}
        for step in range(6):
            a, b, c = step, step - 1, step - 2
            parts = []
            for n in range(8):
                if a < 4:
                    scores(a, n)
                if 0 <= b < 4:
                    parts.append(weigh(b, n))
                if 0 <= c and n % 4 == 0:
                    values(c, n // 4, inv[c])
            if 0 <= b < 4:
                top = jnp.concatenate([x[0] for x in parts], axis=0)
                total = jnp.concatenate([x[1] for x in parts], axis=0)
                inv[b] = 1.0 / total
                lse = top * SCALE + jnp.log(total)
                hi = lse.astype(BF).astype(F32)
                mid = (lse - hi).astype(BF).astype(F32)
                lo = lse - hi - mid
                for e in range(4):
                    at = slice(e * 128 + (b % 2) * 64, e * 128 + (b % 2) * 64 + 64)
                    row = pst[at]
                    for n, part in enumerate((hi, mid, lo)):
                        at_lane = n * 32 + (b // 2) * 16 + e * 4 + i
                        row = jnp.where(lane64 == at_lane, part[e * 64 : e * 64 + 64], row)
                    pst[at] = row
            if c in (1, 3):
                par = c // 2
                for e in range(4):
                    rows = slice(e * 64, e * 64 + 64)
                    lhs = jnp.concatenate([ob[0, rows], ob[1, rows]], axis=0)
                    v = dot(lhs, wuv_v[e * 8 + 2 * i + par])
                    vq[e * 128 : e * 128 + 128, par * 128 : par * 128 + 128] = v.astype(BF)
        for b in range(4):
            z = dot(slotst_v[b * 128 : b * 128 + 128], vq[...])
            bs[i, b * 8 : b * 8 + 8] = z.astype(BF).reshape(8, 16, 256)
        x_send(*backward(i))

    srow, slane = iota((128, 128), 0), iota((128, 128), 1)

    def suffix(c):
        with jax.named_scope("wait_y"):
            for par in range(2):
                for k in range(1, TP):
                    y_copy(k, par, c).wait_recv()
        lane = iota((16, 128), 1)
        spos = iota((128, SLEN), 1)

        def match(j):
            r = c * 4 + j
            ql = jnp.concatenate([yrlat[k, r] for k in range(TP)], axis=0)
            parts = []
            for k in range(TP):
                x = yrrope[k, r]
                zero = jnp.zeros_like(x)
                parts += [jnp.where(lane < 64, x, zero), jnp.where(lane >= 64, x, zero)]
            s = lax.dot_general(ql, sl_v[r], (((1,), (1,)), ((), ())), preferred_element_type=F32)
            ss[j] = s + dot(jnp.concatenate(parts, axis=0), skr_v[r])

        def soft(j):
            r = c * 4 + j
            live = spos < slen[0, t * OWN + r]
            s = jnp.where(live, ss[j], -1e30)
            top = jnp.max(s, axis=1, keepdims=True)
            e = jnp.where(live, jnp.exp2((s - top) * SCALE2), 0.0)
            total = jnp.sum(e, axis=1, keepdims=True)
            es[j] = e.astype(BF)
            lse = top * SCALE + jnp.log(total)
            stat_v[...] = jnp.where(slane == (srow >> 5) * OWN + r, lse, stat_v[...])
            return 1.0 / total

        def mixed(j, inv):
            r = c * 4 + j
            for n in range(2):
                at = pl.ds(n * 256, 256)
                o = (dot(es[j], sl_v[r, :, at]) * inv).astype(BF)
                for k in range(TP):
                    o_v[k, r, :, at] = o[k * 32 : k * 32 + 32]

        inv = {}
        for step in range(6):
            if step < 4:
                match(step)
            if 0 <= step - 1 < 4:
                inv[step - 1] = soft(step - 1)
            if 0 <= step - 2:
                mixed(step - 2, inv[step - 2])

    def yb_copy(k, rh, q):
        at = pl.ds(q * 4, 4)
        n = (k - 1) * 8 + rh * 4 + q
        return pltpu.make_async_remote_copy(
            src_ref=ybs.at[k - 1, rh, at], dst_ref=ybr.at[k, rh, at],
            send_sem=bss.at[n], recv_sem=brs.at[n], device_id=y_back(k), device_id_type=MESH,
        )

    def yb_stat_copy(k):
        return pltpu.make_async_remote_copy(
            src_ref=ybs_st.at[k - 1], dst_ref=ybr_st.at[k],
            send_sem=bsts.at[k - 1], recv_sem=brts.at[k - 1], device_id=y_back(k), device_id_type=MESH,
        )

    def return_half(rh):
        for k in (1, 2, 3, 0):
            for n in range(2):
                cut = o_v[k, pl.ds(rh * 8, 8), :, n * 256 : n * 256 + 256].reshape(256, 256)
                z = dot(permb_v[...], cut).astype(BF).reshape(16, 16, 256)
                if k == 0:
                    ybr[0, rh, :, :, n * 256 : n * 256 + 256] = z
                else:
                    ybs[k - 1, rh, :, :, n * 256 : n * 256 + 256] = z
            if k == 3:
                for q in range(4):
                    for m in range(1, TP):
                        yb_copy(m, rh, q).start()

    with jax.named_scope("wait_rope"):
        for c in ropes:
            c.wait_recv()

    def attend(j, carry):
        with jax.named_scope("quarter"):
            quarter(j)
        with jax.named_scope("suffix"):
            suffix(j)
        return carry

    def attend_suffix(j, carry):
        with jax.named_scope("suffix"):
            suffix(j)
        return carry

    def attend_prefix(j, carry):
        with jax.named_scope("quarter"):
            quarter(j)
        return carry

    lax.fori_loop(0, 2, attend, 0)
    with jax.named_scope("yback"):
        return_half(0)
    lax.fori_loop(2, 4, attend_suffix, 0)
    for k in range(TP):
        part = stat_v[k * 32 : k * 32 + 32]
        if k == 0:
            ybr_st[0] = part
        else:
            ybs_st[k - 1] = part
    stats = [yb_stat_copy(k) for k in range(1, TP)]
    for c in stats:
        c.start()
    with jax.named_scope("yback"):
        return_half(1)
    lax.fori_loop(2, 4, attend_prefix, 0)
    for b in range(4):
        z = dot(slotst_v[b * 128 : b * 128 + 128], pst[...].astype(BF))
        bs_st[b * 8 : b * 8 + 8] = z.astype(BF).reshape(8, 16, STATS)
    x_send(*back_stats)

    def prefix_part(i):
        with jax.named_scope("wait_x_back"):
            x_all(*backward(i)).wait_recv()
        pv_v[i] = dot(selt_v[...], br[i].reshape(512, 256))

    def suffix_part(q):
        with jax.named_scope("wait_yback"):
            for rh in range(2):
                for k in range(1, TP):
                    yb_copy(k, rh, q).wait_recv()
        for hp in range(q * 4, q * 4 + 4):
            lhs = jnp.concatenate([ybr[k, rh, hp] for k in range(TP) for rh in range(2)], axis=0)
            rhs = jnp.concatenate([wuv_v[2 * hp], wuv_v[2 * hp + 1]], axis=1)
            sv = dot(lhs, rhs)
            for par in range(2):
                h = 2 * hp + par
                sv_v[:, h * 128 : h * 128 + 128] = jnp.concatenate(
                    [sv[e * 16 + par * 8 : e * 16 + par * 8 + 8, par * 128 : par * 128 + 128] for e in range(8)],
                    axis=0,
                ).astype(BF)

    with jax.named_scope("parts"):
        for i in range(QUARTERS - 1):
            prefix_part(i)
            suffix_part(i)
    with jax.named_scope("wait_stats"):
        x_all(*back_stats).wait_recv()
        for c in stats:
            c.wait_recv()
    st = ybr_st[0] + ybr_st[1] + ybr_st[2] + ybr_st[3]
    ls = jnp.concatenate([st, jnp.zeros((96, 128), F32)], axis=0).T[0:64]
    lp = jnp.zeros((64, 128), F32)
    for c in range(4):
        lp = lp + dot(selt_v[c * 64 : c * 64 + 64], br_st[...].reshape(512, STATS))
    lp = lp + pltpu.roll(lp, 96, 1) + pltpu.roll(lp, 64, 1)
    top = jnp.maximum(lp, ls)
    a, b = jnp.exp(lp - top), jnp.exp(ls - top)
    inv = 1.0 / (a + b)
    a, b = a * inv, b * inv
    with jax.named_scope("last"):
        prefix_part(QUARTERS - 1)
        suffix_part(3)
    outs = []
    for q in range(4):
        with jax.named_scope("finish"):
            for hl in range(8):
                h, i, par = q * 8 + hl, hl // 2, hl % 2
                at, col = slice(h * 128, h * 128 + 128), par * 16 + h // 2
                prefix = pv_v[i, q * 64 : q * 64 + 64, par * 128 : par * 128 + 128]
                own = sv_v[:, at].astype(F32)
                out_v[:, at] = (a[:, col : col + 1] * prefix + b[:, col : col + 1] * own).astype(BF)
            for k in range(TP):
                c = pltpu.make_async_copy(
                    out_v.at[pl.ds(k * OWN, OWN), pl.ds(q * 1024, 1024)],
                    out.at[pl.ds(rel(k), OWN), pl.ds(q * 1024, 1024)],
                    osem.at[q * 4 + k],
                )
                c.start()
                outs.append(c)
    with jax.named_scope("wait_sends"):
        for k in range(1, TP):
            for c in range(4):
                for par in range(2):
                    y_copy(k, par, c).wait_send()
                    yb_copy(k, par, c).wait_send()
        for c in (*ropes, *stats):
            c.wait_send()
        for i in range(QUARTERS):
            x_all(*forward(i)).wait_send()
            x_all(*backward(i)).wait_send()
        x_all(*back_stats).wait_send()
    with jax.named_scope("waitout"):
        for c in outs:
            c.wait()


def local(qn, qr, wuk, wuv, plat, prope, slat, srope, slen, named, slot):
    hbm = pl.BlockSpec(memory_space=pl.ANY)
    smem = pl.BlockSpec(memory_space=pltpu.SMEM)

    def b(*shape):
        return pltpu.VMEM(shape, BF)

    def f(*shape):
        return pltpu.VMEM(shape, F32)

    def sem(n):
        return pltpu.SemaphoreType.DMA((n,))

    return pl.pallas_call(
        kernel,
        out_shape=jax.ShapeDtypeStruct((REQS, HEADS * VALUE), BF),
        in_specs=[hbm] * 8 + [smem] * 3,
        out_specs=hbm,
        scratch_shapes=[
            b(64, 4096), b(64, 2048), b(32, 128, 512), b(32, 512, 128), b(2, 2048, 512), b(2, 640, 2048),
            b(16, 256, 512), b(16, 128, 256),
            b(512, 256), b(256, 512), b(256, 256), b(256, 256), b(512, 512), b(512, 512),
            b(4, 16, 16, 512), b(3, 16, 32, 512), b(4, 16, 32, 512), b(3, 16, 16, 128), b(4, 16, 16, 128),
            b(4, 16, 32, 512), b(3, 2, 16, 16, 512), b(4, 2, 16, 16, 512),
            f(128, 128), f(3, 32, 128), f(4, 32, 128),
            b(4, 32, 16, 384), b(4, 32, 16, 384), b(512, 384), b(512, 256), f(512, 128),
            b(4, 32, 16, 256), b(4, 32, 16, 256), b(32, 16, STATS), b(32, 16, STATS),
            b(4, 256, 640), f(2, 256, 2048), b(2, 256, 2048), b(2, 256, 512),
            f(4, 128, 256), b(4, 128, 256), f(4, 256, 256), b(64, 4096), b(64, 4096),
            sem(13), sem(16), sem(24), sem(24), sem(3), sem(3), sem(24), sem(24), sem(3), sem(3),
            sem(4), sem(4), sem(5), sem(5),
        ],
        compiler_params=pltpu.CompilerParams(
            collective_id=0, has_side_effects=True, vmem_limit_bytes=67043328
        ),
        name="attend",
    )(qn, qr, wuk, wuv, plat, prope, slat, srope, named, slot, slen)


def solution(mesh):
    in_specs = (
        P("grp", "tp"), P("grp", "tp"), P("tp", None, None), P("tp", None, None),
        P("grp", None, None), P("grp", None, None), P(("grp", "tp"), None, None), P(("grp", "tp"), None, None),
        P("grp", None), P("grp"), P(),
    )
    return jax.shard_map(local, mesh=mesh, in_specs=in_specs, out_specs=P("grp", "tp"), check_vma=False)
```

time: 92 us -> 71.2 us (0.77)
  Pallas kernels: 86.6 us -> 69.1 us
  local copies, waits for them, and re-layouts: 4.54 us -> 1.87 us
    pallas_call x1, Pallas kernels: 86.6 us -> 69.1 us  [local(): pl.pallas_call(kernel, out_shape=jax.ShapeDtypeStruct((REQS, HEADS * VALU...]
    broadcast_in_dim x4 -> x0, local copies, waits for them, and re-layouts: 1.36 us -> none  [the longest x2 0.68 us: local(): ps = jnp.broadcast_to(jnp.tile(slot, 2)[None], (8, 128))]
    another operation x2 -> x0, local copies, waits for them, and re-layouts: 1.31 us -> none  [the longest x1 0.66 us: local(): rp = jnp.broadcast_to(jnp.tile(named, 2)[None], (8, 128))]
where the time goes in v1:
time: 71.2 us; the launch traced here: 71 us
  Pallas kernels  69.1 us (97%)
  local copies, waits for them, and re-layouts  1.87 us (3%)
    pallas_call x1, Pallas kernels, local(): pl.pallas_call(kernel, out_shape=jax.ShapeDtypeStruct((REQS, HEADS * VALU...  69.1 us
    unnamed x1, local copies, waits for them, and re-layouts  1.87 us

profile of v1, /device:TPU:1, one launch (start us, length us, event | category | flops | bytes accessed | tf_op | source)
XLA Modules:
  0.0 71.0 jit_solution(1001087082168321364)
XLA Ops:
  0.0 69.1 %attend.1 = bf16[64,4096]{1,0:T(8,128)(2,1)} custom-call(bf16[64,4096]{1,0:T(8,128)(2,1)} %qn.1, bf16[64,2048]{1,0:T(8,128)(2,1)} %qr.1, bf16[32,128,512]{2,1,0:T(8,128)(2,1)} %wuk.1, bf16[32,512,128]{2,1,0:T(8,128)(2,1)} %wuv.1, bf16[2,2048,512]{2,1,0:T(8,128)(2,1)} %plat.1, bf16[2,64,2048]{2,1,0:T(8,128)(2,1)} %prope.1, bf16[16,256,512]{2,1,0:T(8,128)(2,1)} %slat.1, ...), custom_call_target="tpu_custom_call" | custom-call | tf_op jit(solution)/shard_map/attend/pallas_call | solution.py:539
  69.1 1.9 %copy.13 = bf16[64,4096]{1,0:T(8,128)(2,1)} copy(bf16[64,4096]{1,0:T(8,128)(2,1)} %attend.1) | data formatting | bytes 1048576

commit v2 on v1

--- a/solution.py
+++ b/solution.py
@@ -35,7 +35,7 @@
     qn_v, qr_v, wuk_v, wuv_v, pl_v, kt_v, sl_v, skr_v,
     sel_v, selt_v, perm_v, permb_v, slots_v, slotst_v,
     xlat_v, yslat, yrlat, ysrope, yrrope, o_v, ybs, ybr, stat_v, ybs_st, ybr_st,
-    xs, xr, qp, vq, pst, bs, br, bs_st, br_st,
+    xs, xr, qp, vq, pst, bs, br, bs_c, br_c, bs_a, br_a, bs_b, br_b,
     qb, sc, pb, ob, ss, es, pv_v, sv_v, out_v,
     lsem, osem, yss, yrs, yrss, yrrs, bss, brs, bsts, brts, xss, xrs, zss, zrs,
 ):
@@ -47,7 +47,7 @@
         rows = pl.ds(k * OWN, OWN)
         pltpu.make_async_copy(qn.at[pl.ds(rel(k), OWN)], qn_v.at[rows], lsem.at[0]).start()
         pltpu.make_async_copy(qr.at[pl.ds(rel(k), OWN)], qr_v.at[rows], lsem.at[1]).start()
-    loads = [(wuk, wuk_v)]
+    loads = [(wuk.at[:, b], wuk_v.at[:, b]) for b in range(2)]
     for p in range(2):
         loads.append((plat.at[p], pl_v.at[p]))
         for b in range(2):
@@ -62,15 +62,12 @@
     for k in range(1, TP):
         pl.semaphore_signal(bar, inc=1, device_id=(g, lax.rem(t + k, TP)), device_id_type=MESH)
 
-    def greet(k, c):
+    for k in range(1, GROUPS):
         pl.semaphore_signal(bar, inc=1, device_id=(lax.rem(g + k, GROUPS), t), device_id_type=MESH)
-        return c
-
-    lax.fori_loop(1, GROUPS, greet, 0)
 
     for c in copies[1:]:
         c.start()
-    ld_wuk, ld_p, ld_s, ld_wuv = copies[0], (copies[1:4], copies[4:7]), copies[7:10], copies[10]
+    ld_wuk, ld_p, ld_s, ld_wuv = copies[0:2], copies[2:8], copies[8:11], copies[11]
 
     i, j = iota((256, 256), 0), iota((256, 256), 1)
     perm_v[...] = onehot(j == (i & 15) * 16 + (i >> 4))
@@ -79,9 +76,12 @@
         def one(hp, c):
             h = 2 * hp + par
             q = qn_v[:, pl.ds(pl.multiple_of(h * NOPE, NOPE), NOPE)]
-            y = dot(q, wuk_v[h]).astype(BF)
+            y = dot(q, wuk_v[hp, par]).astype(BF)
             for k in range(TP):
                 xlat_v[k, hp] = y[k * OWN : k * OWN + OWN]
+            if par:
+                p, at = hp // 8, pl.multiple_of((hp % 8) * 256, 256)
+                kt_v[p, 0:LATENT, pl.ds(at, 256)] = pl_v[p, pl.ds(at, 256), :].T
             return c
 
         lax.fori_loop(0, 16, one, 0, unroll=4)
@@ -95,23 +95,6 @@
                 else:
                     yslat[k - 1, :, half, n * 256 : n * 256 + 256] = z
 
-    with jax.named_scope("wait_q"):
-        pltpu.make_async_copy(qn, qn_v, lsem.at[0]).wait()
-        pltpu.make_async_copy(qr, qr_v, lsem.at[1]).wait()
-    with jax.named_scope("ropes"):
-        for k in range(TP):
-            rope = jnp.concatenate(
-                [qr_v[k * OWN : k * OWN + OWN, hp * 128 : hp * 128 + 128] for hp in range(16)], axis=0
-            )
-            z = dot(perm_v[...], rope).astype(BF).reshape(16, 16, 128)
-            if k == 0:
-                yrrope[0] = z
-            else:
-                ysrope[k - 1] = z
-    ld_wuk.wait()
-    with jax.named_scope("qlat0"):
-        q_latents(0)
-
     def y_to(k):
         return (g, lax.rem(t + k, TP))
 
@@ -127,22 +110,20 @@
             send_sem=yss.at[n], recv_sem=yrs.at[n], device_id=y_to(k), device_id_type=MESH,
         )
 
-    def y_rope_copy(k):
+    def y_rope_copy(k, c):
+        at, n = pl.ds(c * 4, 4), (k - 1) * 4 + c
         return pltpu.make_async_remote_copy(
-            src_ref=ysrope.at[k - 1], dst_ref=yrrope.at[k],
-            send_sem=yrss.at[k - 1], recv_sem=yrrs.at[k - 1], device_id=y_to(k), device_id_type=MESH,
+            src_ref=ysrope.at[k - 1, at], dst_ref=yrrope.at[k, at],
+            send_sem=yrss.at[n], recv_sem=yrrs.at[n], device_id=y_to(k), device_id_type=MESH,
         )
 
     def x_send(src, dst, ss, rs):
-        def one(k, c):
+        for k in range(1, GROUPS):
             d = lax.rem(g + k, GROUPS)
             pltpu.make_async_remote_copy(
                 src_ref=src.at[d], dst_ref=dst.at[g],
                 send_sem=ss, recv_sem=rs, device_id=(d, t), device_id_type=MESH,
             ).start()
-            return c
-
-        lax.fori_loop(1, GROUPS, one, 0)
         dst[g] = src[g]
 
     def x_all(src, dst, ss, rs):
@@ -155,18 +136,20 @@
     def forward(i):
         return xs.at[i], xr.at[i], xss.at[i], xrs.at[i]
 
-    def backward(i):
-        return bs.at[i], br.at[i], zss.at[i], zrs.at[i]
-
-    back_stats = (bs_st, br_st, zss.at[QUARTERS], zrs.at[QUARTERS])
-
-    with jax.named_scope("barrier"):
-        pl.semaphore_wait(bar, TP - 1 + GROUPS - 1)
-    ropes = [y_rope_copy(k) for k in range(1, TP)]
-    for c in ropes:
-        c.start()
-    for k in range(1, TP):
-        y_copy(k, 0, 0).start()
+    back_first = (bs, br, zss.at[0], zrs.at[0])
+    back_second = (bs_c, br_c, zss.at[1], zrs.at[1])
+    back_a = (bs_a, br_a, zss.at[3], zrs.at[3])
+    back_b = (bs_b, br_b, zss.at[4], zrs.at[4])
+
+    def place(i):
+        for src, wide, at in ((qn_v, 256, 0), (qr_v, 128, 256)):
+            rhs = jnp.concatenate(
+                [src[:, (c * 4 + i) * wide : (c * 4 + i) * wide + wide] for c in range(4)], axis=0
+            )
+            for b in range(2):
+                got = dot(sel_v[b * 256 : b * 256 + 256], rhs).astype(BF)
+                xs[i, b * 16 : b * 16 + 16, :, at : at + wide] = got.reshape(16, 16, wide)
+
     with jax.named_scope("route"):
         sq = (128, 128)
         first = iota(sq, 0)
@@ -188,25 +171,6 @@
                 sel_v[b * 128 : b * 128 + 128, e * 128 : e * 128 + 128] = onehot(
                     (key == buf_r) & (col == ((j + e * 128) >> 6))
                 )
-
-    with jax.named_scope("place"):
-        for hf in range(QUARTERS):
-            for src, wide, at in ((qn_v, 256, 0), (qr_v, 128, 256)):
-                rhs = jnp.concatenate(
-                    [src[:, (c * 4 + hf) * wide : (c * 4 + hf) * wide + wide] for c in range(4)], axis=0
-                )
-                for b in range(4):
-                    got = dot(sel_v[b * 128 : b * 128 + 128], rhs).astype(BF)
-                    xs[hf, b * 8 : b * 8 + 8, :, at : at + wide] = got.reshape(8, 16, wide)
-            x_send(*forward(hf))
-    with jax.named_scope("qlat1"):
-        q_latents(1)
-    for c in range(4):
-        for par in range(2):
-            for k in range(1, TP):
-                if c or par:
-                    y_copy(k, par, c).start()
-
     with jax.named_scope("masks"):
         for b in range(4):
             i, j = iota((128, 512), 0) + b * 128, iota((128, 512), 1)
@@ -223,19 +187,46 @@
                 )
         i, j = iota((256, 256), 0), iota((256, 256), 1)
         permb_v[...] = onehot(j == (i & 7) * 32 + ((i >> 3) & 1) * 16 + (i >> 4))
-
-    with jax.named_scope("turn"):
-        for p in range(2):
-            for c in ld_p[p]:
-                c.wait()
-
-            def turn(j, c, p=p):
-                at = pl.multiple_of(j * 256, 256)
-                kt_v[p, 0:LATENT, pl.ds(at, 256)] = pl_v[p, pl.ds(at, 256), :].T
-                return c
-
-            lax.fori_loop(0, PLEN // 256, turn, 0)
-
+    with jax.named_scope("wait_q"):
+        pltpu.make_async_copy(qn, qn_v, lsem.at[0]).wait()
+        pltpu.make_async_copy(qr, qr_v, lsem.at[1]).wait()
+    with jax.named_scope("ropes"):
+        for k in range(TP):
+            rope = jnp.concatenate(
+                [qr_v[k * OWN : k * OWN + OWN, hp * 128 : hp * 128 + 128] for hp in range(16)], axis=0
+            )
+            z = dot(perm_v[...], rope).astype(BF).reshape(16, 16, 128)
+            if k == 0:
+                yrrope[0] = z
+            else:
+                ysrope[k - 1] = z
+    with jax.named_scope("place0"):
+        place(0)
+    with jax.named_scope("barrier"):
+        pl.semaphore_wait(bar, TP - 1 + GROUPS - 1)
+    for c in range(4):
+        for k in range(1, TP):
+            y_rope_copy(k, c).start()
+    x_send(*forward(0))
+    ld_wuk[0].wait()
+    with jax.named_scope("qlat0"):
+        q_latents(0)
+    for k in range(1, TP):
+        y_copy(k, 0, 0).start()
+    with jax.named_scope("place"):
+        for i in range(1, QUARTERS):
+            place(i)
+    for c in (ld_wuk[1], *ld_p):
+        c.wait()
+    with jax.named_scope("qlat1"):
+        q_latents(1)
+    for c in range(4):
+        for par in range(2):
+            for k in range(1, TP):
+                if c or par:
+                    y_copy(k, par, c).start()
+
+    x_send(*forward(1))
     pst[...] = jnp.zeros_like(pst)
     stat_v[...] = jnp.zeros_like(stat_v)
     lane64 = iota((64, 128), 1)
@@ -270,20 +261,26 @@
         at = pl.ds(n * 256, 256)
         ob[b % 2, :, at] = (dot(pb[b % 2], pl_v[b % 2, :, at]) * inv).astype(BF)
 
-    def quarter(i):
+    def give_back(rows, to, wide):
+        for b in range(2):
+            z = dot(slotst_v[b * 256 : b * 256 + 256], rows)
+            to[b * 16 : b * 16 + 16] = z.astype(BF).reshape(16, 16, wide)
+
+    def quarter(i, final=False):
         with jax.named_scope("wait_x"):
             x_all(*forward(i)).wait_recv()
-        for b in range(4):
+        if not isinstance(i, int):
+            x_send(*forward(i + 2))
+        for b in range(2):
             for at, wide in ((0, 256), (256, 128)):
                 cut = xr[i, :, :, at : at + wide].reshape(512, wide)
-                qp[b * 128 : b * 128 + 128, at : at + wide] = dot(
-                    slots_v[b * 128 : b * 128 + 128], cut
-                ).astype(BF)
+                rows = slice(b * 256, b * 256 + 256)
+                qp[rows, at : at + wide] = dot(slots_v[rows], cut).astype(BF)
         lane = iota((128, 128), 1)
         for par in range(2):
             for c in range(4):
                 rows = slice(c * 128, c * 128 + 128)
-                y = dot(qp[rows, par * 128 : par * 128 + 128], wuk_v[c * 8 + 2 * i + par]).astype(BF)
+                y = dot(qp[rows, par * 128 : par * 128 + 128], wuk_v[c * 4 + i, par]).astype(BF)
                 r = qp[rows, 256:384]
                 r = jnp.where((lane < 64) if par == 0 else (lane >= 64), r, jnp.zeros_like(r))
                 for p in range(2):
@@ -322,10 +319,20 @@
                     lhs = jnp.concatenate([ob[0, rows], ob[1, rows]], axis=0)
                     v = dot(lhs, wuv_v[e * 8 + 2 * i + par])
                     vq[e * 128 : e * 128 + 128, par * 128 : par * 128 + 128] = v.astype(BF)
-        for b in range(4):
-            z = dot(slotst_v[b * 128 : b * 128 + 128], vq[...])
-            bs[i, b * 8 : b * 8 + 8] = z.astype(BF).reshape(8, 16, 256)
-        x_send(*backward(i))
+                if final and par == 0:
+                    give_back(vq[:, 0:128], bs_a, 128)
+                    x_send(*back_a)
+        if final:
+            give_back(jnp.concatenate([vq[:, 128:256], pst[...].astype(BF)], axis=1), bs_b, 256)
+            x_send(*back_b)
+        elif isinstance(i, int):
+            give_back(vq[...], bs_c, 256)
+            x_send(*back_second)
+        else:
+            for b in range(2):
+                z = dot(slotst_v[b * 256 : b * 256 + 256], vq[...])
+                at = pl.ds(pl.multiple_of(i * 256, 256), 256)
+                bs[b * 16 : b * 16 + 16, :, at] = z.astype(BF).reshape(16, 16, 256)
 
     srow, slane = iota((128, 128), 0), iota((128, 128), 1)
 
@@ -334,6 +341,8 @@
             for par in range(2):
                 for k in range(1, TP):
                     y_copy(k, par, c).wait_recv()
+            for k in range(1, TP):
+                y_rope_copy(k, c).wait_recv()
         lane = iota((16, 128), 1)
         spos = iota((128, SLEN), 1)
 
@@ -405,10 +414,6 @@
                     for m in range(1, TP):
                         yb_copy(m, rh, q).start()
 
-    with jax.named_scope("wait_rope"):
-        for c in ropes:
-            c.wait_recv()
-
     def attend(j, carry):
         with jax.named_scope("quarter"):
             quarter(j)
@@ -421,14 +426,12 @@
             suffix(j)
         return carry
 
-    def attend_prefix(j, carry):
-        with jax.named_scope("quarter"):
-            quarter(j)
-        return carry
-
     lax.fori_loop(0, 2, attend, 0)
     with jax.named_scope("yback"):
         return_half(0)
+    x_send(*back_first)
+    with jax.named_scope("quarter"):
+        quarter(2)
     lax.fori_loop(2, 4, attend_suffix, 0)
     for k in range(TP):
         part = stat_v[k * 32 : k * 32 + 32]
@@ -441,16 +444,18 @@
         c.start()
     with jax.named_scope("yback"):
         return_half(1)
-    lax.fori_loop(2, 4, attend_prefix, 0)
-    for b in range(4):
-        z = dot(slotst_v[b * 128 : b * 128 + 128], pst[...].astype(BF))
-        bs_st[b * 8 : b * 8 + 8] = z.astype(BF).reshape(8, 16, STATS)
-    x_send(*back_stats)
+    with jax.named_scope("quarter"):
+        quarter(3, True)
 
     def prefix_part(i):
-        with jax.named_scope("wait_x_back"):
-            x_all(*backward(i)).wait_recv()
-        pv_v[i] = dot(selt_v[...], br[i].reshape(512, 256))
+        if i == 2:
+            x_all(*back_second).wait_recv()
+            back = br_c[...]
+        else:
+            if i == 0:
+                x_all(*back_first).wait_recv()
+            back = br[:, :, i * 256 : i * 256 + 256]
+        pv_v[i] = dot(selt_v[...], back.reshape(512, 256))
 
     def suffix_part(q):
         with jax.named_scope("wait_yback"):
@@ -471,54 +476,69 @@
     with jax.named_scope("parts"):
         for i in range(QUARTERS - 1):
             prefix_part(i)
+        for i in range(QUARTERS - 1):
             suffix_part(i)
     with jax.named_scope("wait_stats"):
-        x_all(*back_stats).wait_recv()
         for c in stats:
             c.wait_recv()
     st = ybr_st[0] + ybr_st[1] + ybr_st[2] + ybr_st[3]
     ls = jnp.concatenate([st, jnp.zeros((96, 128), F32)], axis=0).T[0:64]
+    with jax.named_scope("wait_last"):
+        x_all(*back_a).wait_recv()
+        x_all(*back_b).wait_recv()
+    pv_v[3, :, 0:128] = dot(selt_v[...], br_a[...].reshape(512, 128))
+    last = dot(selt_v[...], br_b[...].reshape(512, 256))
+    pv_v[3, :, 128:256] = last[:, 0:128]
     lp = jnp.zeros((64, 128), F32)
     for c in range(4):
-        lp = lp + dot(selt_v[c * 64 : c * 64 + 64], br_st[...].reshape(512, STATS))
+        lp = lp + last[c * 64 : c * 64 + 64, 128:256]
     lp = lp + pltpu.roll(lp, 96, 1) + pltpu.roll(lp, 64, 1)
     top = jnp.maximum(lp, ls)
     a, b = jnp.exp(lp - top), jnp.exp(ls - top)
     inv = 1.0 / (a + b)
     a, b = a * inv, b * inv
+    outs = []
+
+    def finish(q):
+        for h in range(q * 8, q * 8 + 8):
+            i, par = h % 8 // 2, h % 2
+            at, col = slice(h * 128, h * 128 + 128), par * 16 + h // 2
+            prefix = pv_v[i, q * 64 : q * 64 + 64, par * 128 : par * 128 + 128]
+            own = sv_v[:, at].astype(F32)
+            out_v[:, at] = (a[:, col : col + 1] * prefix + b[:, col : col + 1] * own).astype(BF)
+        for k in range(TP):
+            c = pltpu.make_async_copy(
+                out_v.at[pl.ds(k * OWN, OWN), pl.ds(q * 1024, 1024)],
+                out.at[pl.ds(rel(k), OWN), pl.ds(q * 1024, 1024)],
+                osem.at[q * 4 + k],
+            )
+            c.start()
+            outs.append(c)
+
+    with jax.named_scope("finish"):
+        for q in range(3):
+            finish(q)
     with jax.named_scope("last"):
-        prefix_part(QUARTERS - 1)
         suffix_part(3)
-    outs = []
-    for q in range(4):
-        with jax.named_scope("finish"):
-            for hl in range(8):
-                h, i, par = q * 8 + hl, hl // 2, hl % 2
-                at, col = slice(h * 128, h * 128 + 128), par * 16 + h // 2
-                prefix = pv_v[i, q * 64 : q * 64 + 64, par * 128 : par * 128 + 128]
-                own = sv_v[:, at].astype(F32)
-                out_v[:, at] = (a[:, col : col + 1] * prefix + b[:, col : col + 1] * own).astype(BF)
-            for k in range(TP):
-                c = pltpu.make_async_copy(
-                    out_v.at[pl.ds(k * OWN, OWN), pl.ds(q * 1024, 1024)],
-                    out.at[pl.ds(rel(k), OWN), pl.ds(q * 1024, 1024)],
-                    osem.at[q * 4 + k],
-                )
-                c.start()
-                outs.append(c)
+        finish(3)
     with jax.named_scope("wait_sends"):
         for k in range(1, TP):
             for c in range(4):
                 for par in range(2):
                     y_copy(k, par, c).wait_send()
                     yb_copy(k, par, c).wait_send()
-        for c in (*ropes, *stats):
+        for k in range(1, TP):
+            for c in range(4):
+                y_rope_copy(k, c).wait_send()
+        for c in stats:
             c.wait_send()
         for i in range(QUARTERS):
             x_all(*forward(i)).wait_send()
-            x_all(*backward(i)).wait_send()
-        x_all(*back_stats).wait_send()
-    with jax.named_scope("waitout"):
+        x_all(*back_first).wait_send()
+        x_all(*back_second).wait_send()
+        x_all(*back_a).wait_send()
+        x_all(*back_b).wait_send()
+    with jax.named_scope("wait_out"):
         for c in outs:
             c.wait()
 
@@ -542,24 +562,24 @@
         in_specs=[hbm] * 8 + [smem] * 3,
         out_specs=hbm,
         scratch_shapes=[
-            b(64, 4096), b(64, 2048), b(32, 128, 512), b(32, 512, 128), b(2, 2048, 512), b(2, 640, 2048),
+            b(64, 4096), b(64, 2048), b(16, 2, 128, 512), b(32, 512, 128), b(2, 2048, 512), b(2, 640, 2048),
             b(16, 256, 512), b(16, 128, 256),
             b(512, 256), b(256, 512), b(256, 256), b(256, 256), b(512, 512), b(512, 512),
             b(4, 16, 16, 512), b(3, 16, 32, 512), b(4, 16, 32, 512), b(3, 16, 16, 128), b(4, 16, 16, 128),
             b(4, 16, 32, 512), b(3, 2, 16, 16, 512), b(4, 2, 16, 16, 512),
             f(128, 128), f(3, 32, 128), f(4, 32, 128),
             b(4, 32, 16, 384), b(4, 32, 16, 384), b(512, 384), b(512, 256), f(512, 128),
-            b(4, 32, 16, 256), b(4, 32, 16, 256), b(32, 16, STATS), b(32, 16, STATS),
+            b(32, 16, 512), b(32, 16, 512), b(32, 16, 256), b(32, 16, 256), b(32, 16, 128), b(32, 16, 128), b(32, 16, 256), b(32, 16, 256),
             b(4, 256, 640), f(2, 256, 2048), b(2, 256, 2048), b(2, 256, 512),
             f(4, 128, 256), b(4, 128, 256), f(4, 256, 256), b(64, 4096), b(64, 4096),
-            sem(13), sem(16), sem(24), sem(24), sem(3), sem(3), sem(24), sem(24), sem(3), sem(3),
+            sem(14), sem(16), sem(24), sem(24), sem(12), sem(12), sem(24), sem(24), sem(3), sem(3),
             sem(4), sem(4), sem(5), sem(5),
         ],
         compiler_params=pltpu.CompilerParams(
             collective_id=0, has_side_effects=True, vmem_limit_bytes=67043328
         ),
         name="attend",
-    )(qn, qr, wuk, wuv, plat, prope, slat, srope, named, slot, slen)
+    )(qn, qr, wuk.reshape(16, 2, NOPE, LATENT), wuv, plat, prope, slat, srope, named, slot, slen)
 
 
 def solution(mesh):

time: 71.2 us -> 67.3 us (0.945)
  Pallas kernels: 69.1 us -> 65.3 us
    pallas_call x1, Pallas kernels: 69.1 us -> 65.3 us  [local(): pl.pallas_call(kernel, out_shape=jax.ShapeDtypeStruct((REQS, HEADS * VALU...]
where the time goes in v2:
time: 67.3 us; the launch traced here: 67.2 us
  Pallas kernels  65.3 us (97%)
  local copies, waits for them, and re-layouts  1.87 us (3%)
    pallas_call x1, Pallas kernels, local(): pl.pallas_call(kernel, out_shape=jax.ShapeDtypeStruct((REQS, HEADS * VALU...  65.3 us
    unnamed x1, local copies, waits for them, and re-layouts  1.87 us

profile of v2, /device:TPU:1, one launch (start us, length us, event | category | flops | bytes accessed | tf_op | source)
XLA Modules:
  0.0 67.2 jit_solution(8859463217473658460)
XLA Ops:
  0.0 65.3 %attend.1 = bf16[64,4096]{1,0:T(8,128)(2,1)} custom-call(bf16[64,4096]{1,0:T(8,128)(2,1)} %qn.1, bf16[64,2048]{1,0:T(8,128)(2,1)} %qr.1, bf16[16,2,128,512]{3,2,1,0:T(8,128)(2,1)} %bitcast.1, bf16[32,512,128]{2,1,0:T(8,128)(2,1)} %wuv.1, bf16[2,2048,512]{2,1,0:T(8,128)(2,1)} %plat.1, bf16[2,64,2048]{2,1,0:T(8,128)(2,1)} %prope.1, ...), custom_call_target="tpu_custom_call" | custom-call | tf_op jit(solution)/shard_map/attend/pallas_call | solution.py:559
  65.3 1.9 %copy.13 = bf16[64,4096]{1,0:T(8,128)(2,1)} copy(bf16[64,4096]{1,0:T(8,128)(2,1)} %attend.1) | data formatting | bytes 1048576
